TPU v7x, 32 devices: a whole 2x2x4 slice. The times are simulated.
32 devices in a mesh: gx: 4 (over y, core), gy: 2 (over x), gz: 4 (over z).
Axes of the slice: x: 2, y: 2, z: 4, core: 2. Of those that a mesh axis runs over, the one named last changes fastest.
Arguments:
- tokens: bfloat16 [32, 6144], P('gy'), may hold values from -6 to 6
- route: int32 [32, 2], P('gy'), may hold values from 0 to 3, all different within a row; in each aligned block of 16 rows (0 to 15, 16 to 31, ...) at most 12 rows name the same one
- weight_q: int32 [32, 2], P('gy'), may hold values from 1 to 65535
- w_gate: bfloat16 [4, 6144, 16384], P('gx', 'gy', 'gz'), may hold values from -0.078125 to 0.078125
- w_up: bfloat16 [4, 6144, 16384], P('gx', 'gy', 'gz'), may hold values from -0.078125 to 0.078125
- w_down: bfloat16 [4, 16384, 6144], P('gx', 'gz', 'gy'), may hold values from -0.046875 to 0.046875
Outputs:
- mixed: bfloat16 [32, 6144], P('gy', ('gx', 'gz'))
Inputs may be any that keep to these rules, and one draw needn't show every extreme that they name: `route`: the 2 entries of a row are different; in each block of 16 rows owned by one index of gy no expert is named by more than 12 rows, a bound that some block reaches.
All inputs are finite; a program needn't handle non-finite values.
Results may differ from a plain program's by a relative error of at most 0.0049.
Values may be sent and summed in bfloat16 or wider, within the bound.
A program may use at most 256 MiB of HBM per device.

v0:
```python
import jax
import jax.numpy as jnp
from jax import lax
from jax.sharding import PartitionSpec as P

CAP = 12


def per_device(tokens, route, weight_q, w_gate, w_up, w_down):
    expert = lax.axis_index("gx")
    width_z = lax.axis_size("gz")
    owners = lax.axis_size("gy")
    hits = (route == expert).astype(jnp.int32)
    routed = jnp.sum(hits, axis=1)
    slot_index = jnp.cumsum(routed) - 1
    columns = jnp.arange(CAP, dtype=jnp.int32)
    placing = (slot_index[None, :] == columns[:, None]) & (routed[None, :] > 0)
    place_half = placing.astype(jnp.bfloat16)
    place_full = placing.astype(jnp.float32)
    outgoing = jnp.dot(place_half, tokens, preferred_element_type=jnp.float32).astype(jnp.bfloat16)
    weights_f = weight_q.astype(jnp.float32)
    shares = weights_f / jnp.sum(weights_f, axis=1, keepdims=True)
    token_gate = jnp.sum(hits.astype(jnp.float32) * shares, axis=1)
    slot_gate = jnp.dot(place_full, token_gate, precision=lax.Precision.HIGHEST)
    depth = w_gate.shape[1]
    half = outgoing.reshape(CAP, owners, depth).transpose(1, 0, 2)
    piece = lax.all_to_all(half, "gy", split_axis=0, concat_axis=0, tiled=True)
    piece = piece.reshape(owners * CAP, depth)
    gate = jnp.dot(piece, w_gate[0], preferred_element_type=jnp.float32)
    upper = jnp.dot(piece, w_up[0], preferred_element_type=jnp.float32)
    both = lax.psum_scatter(jnp.stack([gate, upper]), "gy", scatter_dimension=2, tiled=True)
    hidden = (jax.nn.silu(both[0]) * both[1]).astype(jnp.bfloat16)
    down_local = w_down[0]
    partial_value = jnp.dot(
        lax.all_gather(hidden, "gy", axis=1, tiled=True),
        down_local,
        preferred_element_type=jnp.float32,
    )
    portion = CAP // width_z
    column_width = partial_value.shape[1]
    blocks = partial_value.reshape(owners, width_z, portion, column_width)
    narrowed = lax.psum_scatter(blocks, "gz", scatter_dimension=1, tiled=True)
    arrived = lax.all_to_all(narrowed, "gy", split_axis=0, concat_axis=1, tiled=True)
    full = jnp.transpose(arrived[0], (1, 0, 2)).reshape(portion, owners * column_width)
    first = lax.axis_index("gz") * portion
    gate_part = lax.dynamic_slice_in_dim(slot_gate, first, portion, 0)
    place_part = lax.dynamic_slice_in_dim(place_full, first, portion, 0)
    weighted = gate_part[:, None] * full
    contribution = jnp.dot(place_part.T, weighted, precision=lax.Precision.HIGHEST)
    result = lax.psum_scatter(contribution, ("gx", "gz"), scatter_dimension=1, tiled=True)
    return result.astype(jnp.bfloat16)


def solution(mesh):
    in_specs = (
        P("gy", None),
        P("gy", None),
        P("gy", None),
        P("gx", "gy", "gz"),
        P("gx", "gy", "gz"),
        P("gx", "gz", "gy"),
    )
    out_specs = P("gy", ("gx", "gz"))
    return jax.shard_map(
        per_device, mesh=mesh, in_specs=in_specs, out_specs=out_specs, check_vma=False
    )
```

profile of v0, /device:TPU:0, one launch (start us, length us, event | category | flops | bytes accessed | tf_op | source)
XLA Modules:
  0.0 181.3 jit_solution(7835118890817340249)
XLA Ops:
  6.5 0.7 fusion.21
  7.3 0.1 copy.23
  7.4 0.1 add_reduce_fusion
  7.5 0.2 convolution_convert_fusion
  7.7 0.1 reshape.49
  7.9 8.9 %all_to_all.14 = bf16[2,12,3072]{2,1,0:T(8,128)(2,1)S(1)} all-to-all(bf16[2,12,3072]{2,1,0:T(8,128)(2,1)S(1)} %bitcast.51), channel_id=1, replica_groups=mesh['gx'=4,'gy'=2,'gz'=4] {'gy'}, dimensions={0} | all-to-all | bytes 294912 | tf_op jit(solution)/shard_map/all_to_all | solution.py:27
  16.8 9.9 %fusion.6 = f32[1,24,4096]{2,1,0:T(8,128)S(1)} fusion(bf16[24,3072]{1,0:T(8,128)(2,1)S(1)} %reshape.50, bf16[1,3072,4096]{2,1,0:T(8,128)(2,1)} %param.9), kind=kOutput, calls=%fused_computation.7 | convolution fusion | flops 603979776 | bytes 25706496 | tf_op jit(solution)/shard_map/dot_general | solution.py:29
  26.7 10.0 %fusion.9 = f32[1,24,4096]{2,1,0:T(8,128)S(1)} fusion(bf16[24,3072]{1,0:T(8,128)(2,1)S(1)} %reshape.50, bf16[1,3072,4096]{2,1,0:T(8,128)(2,1)} %param.10), kind=kOutput, calls=%fused_computation.8 | convolution fusion | flops 603979776 | bytes 25706496 | tf_op jit(solution)/shard_map/dot_general | solution.py:30
  36.7 0.9 pad_maximum_fusion
  37.7 0.6 dynamic-slice
  38.3 17.3 %reduce-scatter.3.cloned.1.call-done = f32[2,24,2048]{2,1,0:T(8,128)} async-done(((f32[2,24,4096]{2,1,0:T(8,128)}), f32[2,24,2048]{2,1,0:T(8,128)}) %reduce-scatter.3.cloned.1.call-update) | async-done | bytes 393232 | tf_op jit(solution)/shard_map/reduce_scatter | solution.py:31
  55.6 1.1 fusion.13
  56.7 5.3 %all_gather.3 = bf16[24,4096]{1,0:T(8,128)(2,1)S(1)} all-gather(bf16[24,2048]{1,0:T(8,128)(2,1)S(1)} %fusion.13), channel_id=1, replica_groups=mesh['gx'=4,'gy'=2,'gz'=4] {'gy'}, dimensions={1}, use_global_device_ids=true | all-gather | bytes 294912 | tf_op jit(solution)/shard_map/all_gather | solution.py:35
  62.0 0.1 dot_general.24
  62.1 11.3 %fusion = f32[2,4,3,3072]{3,0,2,1:T(2,128)} fusion(bf16[1,4096,3072]{2,1,0:T(8,128)(2,1)} %param.11, bf16[2,4,3,4096]{3,2,1,0:T(4,128)(2,1)S(1)} %dot_general.24), kind=kOutput, calls=%fused_computation | convolution fusion | flops 603979776 | bytes 25657344 | tf_op jit(solution)/shard_map/dot_general | solution.py:34
  73.5 36.1 %all-reduce.3.cloned.1.call-done = f32[2,4,3,3072]{3,0,2,1:T(2,128)} async-done(((f32[2,4,3,3072]{3,0,2,1:T(2,128)}), f32[2,4,3,3072]{3,0,2,1:T(2,128)}) %all-reduce.3.cloned.1.call-update) | async-done | bytes 294928
  109.6 1.5 constant_dynamic-slice_fusion
  111.1 0.7 copy.27
  111.8 3.3 %all-to-all-start.1 = ((f32[2,1,3,3072]{3,1,2,0:T(1,128)}), f32[2,1,3,3072]{3,1,2,0:T(1,128)S(1)}, u32[]{:S(2)}, u32[]{:S(2)}) async-start(f32[2,1,3,3072]{3,1,2,0:T(1,128)} %copy.27), calls=%async_computation.2 | async-start | bytes 147456 | tf_op jit(solution)/shard_map/all_to_all | solution.py:43
  115.2 0.1 convolution_bitcast_fusion
  115.4 3.9 %all-to-all-done.1 = f32[2,1,3,3072]{3,1,2,0:T(1,128)S(1)} async-done(((f32[2,1,3,3072]{3,1,2,0:T(1,128)}), f32[2,1,3,3072]{3,1,2,0:T(1,128)S(1)}, u32[]{:S(2)}, u32[]{:S(2)}) %all-to-all-start.1) | async-done | bytes 73760 | tf_op jit(solution)/shard_map/all_to_all | solution.py:43
  119.4 1.2 fusion.15
  120.6 52.8 %reduce-scatter.5.cloned.1.call-done = f32[16,384]{1,0:T(8,128)} async-done(((f32[16,6144]{1,0:T(8,128)}), f32[16,384]{1,0:T(8,128)}) %reduce-scatter.5.cloned.1.call-update) | async-done | bytes 24592 | tf_op jit(solution)/shard_map/reduce_scatter | solution.py:50
  173.4 1.3 convert_element_type.25
  (26 shorter events, 0.5 us)
Async XLA Ops:
  6.5 1.0 copy-start
  6.5 49.1 %reduce-scatter.3.cloned.1.call-start = ((), (), s32[]{:S(2)}) async-start(), calls=%async_computation.4 | async-start | bytes 1179648 | tf_op jit(solution)/shard_map/reduce_scatter | solution.py:31
  26.7 11.0 %copy-start.4 = (u32[32]{0:T(128)S(1)}, u32[32]{0:T(128)}, u32[]{:S(2)}) copy-start(u32[32]{0:T(128)} %constant.30) | copy-start | bytes 388
  26.7 11.6 %copy-start.3 = (s32[16,2]{0,1:T(2,128)S(1)}, s32[16,2]{0,1:T(2,128)}, u32[]{:S(2)}) copy-start(s32[16,2]{0,1:T(2,128)} %param.8) | copy-start | bytes 388
  26.7 148.1 %copy-start.1 = (bf16[16,6144]{1,0:T(8,128)(2,1)S(1)}, bf16[16,6144]{1,0:T(8,128)(2,1)}, u32[]{:S(2)}) copy-start(bf16[16,6144]{1,0:T(8,128)(2,1)} %param.6) | copy-start | bytes 589828
  36.7 36.8 %copy-start.2 = (s32[16,2]{0,1:T(2,128)S(1)}, s32[16,2]{0,1:T(2,128)}, u32[]{:S(2)}) copy-start(s32[16,2]{0,1:T(2,128)} %param.7) | copy-start | bytes 388
  37.6 71.9 %all-reduce.3.cloned.1.call-start = ((), (), s32[]{:S(2)}) async-start(), calls=%async_computation.6 | async-start | bytes 589824
  111.8 7.5 %all-to-all-start.1 = ((f32[2,1,3,3072]{3,1,2,0:T(1,128)}), f32[2,1,3,3072]{3,1,2,0:T(1,128)S(1)}, u32[]{:S(2)}, u32[]{:S(2)}) async-start(f32[2,1,3,3072]{3,1,2,0:T(1,128)} %copy.27), calls=%async_computation.2 | async-start | bytes 147456 | tf_op jit(solution)/shard_map/all_to_all | solution.py:43
  115.1 58.3 %reduce-scatter.5.cloned.1.call-start = ((), (), s32[]{:S(2)}) async-start(), calls=%async_computation.5 | async-start | bytes 417792 | tf_op jit(solution)/shard_map/reduce_scatter | solution.py:50
Sparse Core Ops, SparseCore 0:
  37.8 17.8 reduce-scatter.2
  73.6 35.9 all-reduce.2
  120.7 52.6 reduce-scatter.4
where the time goes:
time: 182 us; the launch traced here: 181 us
  waiting for transfers between devices  110 us (60%)
  matrix products  32.7 us (18%)
  blocking collectives  14.1 us (8%)
  between operations  13.2 us (7%)
  other arithmetic  4.3 us (2%)
  starting transfers between devices  3.39 us (2%)
  local copies, waits for them, and re-layouts  3.36 us (2%)
    reduce_scatter x1, waiting for transfers between devices, per_device(): lax.psum_scatter(contribution, ('gx', 'gz'), scatter_dimension=1, tiled=T...  52.8 us
    unnamed x4, waiting for transfers between devices  36.1 us
    reduce_scatter x1, waiting for transfers between devices, per_device(): lax.psum_scatter(jnp.stack([gate, upper]), 'gy', scatter_dimension=2, til...  17.3 us
    dot_general x1, matrix products, per_device(): jnp.dot(lax.all_gather(hidden, 'gy', axis=1, tiled=True), down_local, pre...  11.3 us
    dot_general x1, matrix products, per_device(): upper = jnp.dot(piece, w_up[0], preferred_element_type=jnp.float32)  10 us
    dot_general x1, matrix products, per_device(): gate = jnp.dot(piece, w_gate[0], preferred_element_type=jnp.float32)  9.9 us
    all_to_all x1, blocking collectives, per_device(): piece = lax.all_to_all(half, 'gy', split_axis=0, concat_axis=0, tiled=True)  8.86 us
    all_gather x1, blocking collectives, per_device(): lax.all_gather(hidden, 'gy', axis=1, tiled=True)  5.29 us
  transfers between devices with their start and end apart: 4, of which 4 were waited for; matrix products, arithmetic and copies ran while one was open for 0% of the time, Pallas kernels for 0%

commit v1 on v0

--- a/solution.py
+++ b/solution.py
@@ -40,7 +40,10 @@
     column_width = partial_value.shape[1]
     blocks = partial_value.reshape(owners, width_z, portion, column_width)
     narrowed = lax.psum_scatter(blocks, "gz", scatter_dimension=1, tiled=True)
-    arrived = lax.all_to_all(narrowed, "gy", split_axis=0, concat_axis=1, tiled=True)
+    arrived = jnp.concatenate(
+        lax.all_to_all(jnp.stack(jnp.split(narrowed, lax.axis_size("gy"), axis=0)), "gy", 0, 0),
+        axis=1,
+    )
     full = jnp.transpose(arrived[0], (1, 0, 2)).reshape(portion, owners * column_width)
     first = lax.axis_index("gz") * portion
     gate_part = lax.dynamic_slice_in_dim(slot_gate, first, portion, 0)

time: 182 us -> 182 us (level)
    another operation x1 -> x3, local copies, waits for them, and re-layouts: 0.08 us -> 2.41 us  [the longest x2 2.33 us: per_device(): jnp.stack(jnp.split(narrowed, lax.axis_size('gy'), axis=0))]
where the time goes in v1:
time: 182 us; the launch traced here: 181 us
  waiting for transfers between devices  110 us (60%)
  matrix products  32.7 us (18%)
  blocking collectives  14.1 us (8%)
  between operations  13.2 us (7%)
  other arithmetic  4.37 us (2%)
  local copies, waits for them, and re-layouts  3.48 us (2%)
  starting transfers between devices  3.42 us (2%)
    reduce_scatter x1, waiting for transfers between devices, per_device(): lax.psum_scatter(contribution, ('gx', 'gz'), scatter_dimension=1, tiled=T...  52.7 us
    unnamed x4, waiting for transfers between devices  36.1 us
    reduce_scatter x1, waiting for transfers between devices, per_device(): lax.psum_scatter(jnp.stack([gate, upper]), 'gy', scatter_dimension=2, til...  17.3 us
    dot_general x1, matrix products, per_device(): jnp.dot(lax.all_gather(hidden, 'gy', axis=1, tiled=True), down_local, pre...  11.3 us
    dot_general x1, matrix products, per_device(): upper = jnp.dot(piece, w_up[0], preferred_element_type=jnp.float32)  10 us
    dot_general x1, matrix products, per_device(): gate = jnp.dot(piece, w_gate[0], preferred_element_type=jnp.float32)  9.9 us
    all_to_all x1, blocking collectives, per_device(): piece = lax.all_to_all(half, 'gy', split_axis=0, concat_axis=0, tiled=True)  8.86 us
    all_gather x1, blocking collectives, per_device(): lax.all_gather(hidden, 'gy', axis=1, tiled=True)  5.29 us
  transfers between devices with their start and end apart: 4, of which 4 were waited for; matrix products, arithmetic and copies ran while one was open for 0% of the time, Pallas kernels for 0%

profile of v1, /device:TPU:0, one launch (start us, length us, event | category | flops | bytes accessed | tf_op | source)
XLA Modules:
  0.0 181.5 jit_solution(7842787023278900248)
XLA Ops:
  6.5 0.7 fusion.21
  7.3 0.1 copy.17
  7.4 0.1 add_reduce_fusion
  7.5 0.2 convolution_convert_fusion
  7.7 0.1 reshape.45
  7.9 8.9 %all_to_all.10 = bf16[2,12,3072]{2,1,0:T(8,128)(2,1)S(1)} all-to-all(bf16[2,12,3072]{2,1,0:T(8,128)(2,1)S(1)} %bitcast.55), channel_id=1, replica_groups=mesh['gx'=4,'gy'=2,'gz'=4] {'gy'}, dimensions={0} | all-to-all | bytes 294912 | tf_op jit(solution)/shard_map/all_to_all | solution.py:27
  16.8 9.9 %fusion.6 = f32[1,24,4096]{2,1,0:T(8,128)S(1)} fusion(bf16[24,3072]{1,0:T(8,128)(2,1)S(1)} %reshape.46, bf16[1,3072,4096]{2,1,0:T(8,128)(2,1)} %param.9), kind=kOutput, calls=%fused_computation.7 | convolution fusion | flops 603979776 | bytes 25706496 | tf_op jit(solution)/shard_map/dot_general | solution.py:29
  26.7 10.0 %fusion.9 = f32[1,24,4096]{2,1,0:T(8,128)S(1)} fusion(bf16[24,3072]{1,0:T(8,128)(2,1)S(1)} %reshape.46, bf16[1,3072,4096]{2,1,0:T(8,128)(2,1)} %param.10), kind=kOutput, calls=%fused_computation.8 | convolution fusion | flops 603979776 | bytes 25706496 | tf_op jit(solution)/shard_map/dot_general | solution.py:30
  36.7 0.9 pad_maximum_fusion
  37.7 0.6 dynamic-slice
  38.3 17.3 %reduce-scatter.3.cloned.1.call-done = f32[2,24,2048]{2,1,0:T(8,128)} async-done(((f32[2,24,4096]{2,1,0:T(8,128)}), f32[2,24,2048]{2,1,0:T(8,128)}) %reduce-scatter.3.cloned.1.call-update) | async-done | bytes 393232 | tf_op jit(solution)/shard_map/reduce_scatter | solution.py:31
  55.6 1.1 fusion.13
  56.7 5.3 %all_gather.3 = bf16[24,4096]{1,0:T(8,128)(2,1)S(1)} all-gather(bf16[24,2048]{1,0:T(8,128)(2,1)S(1)} %fusion.13), channel_id=1, replica_groups=mesh['gx'=4,'gy'=2,'gz'=4] {'gy'}, dimensions={1}, use_global_device_ids=true | all-gather | bytes 294912 | tf_op jit(solution)/shard_map/all_gather | solution.py:35
  62.0 0.1 dot_general.24
  62.1 11.3 %fusion = f32[2,4,3,3072]{3,0,2,1:T(2,128)} fusion(bf16[1,4096,3072]{2,1,0:T(8,128)(2,1)} %param.11, bf16[2,4,3,4096]{3,2,1,0:T(4,128)(2,1)S(1)} %dot_general.24), kind=kOutput, calls=%fused_computation | convolution fusion | flops 603979776 | bytes 25657344 | tf_op jit(solution)/shard_map/dot_general | solution.py:34
  73.5 36.1 %all-reduce.3.cloned.1.call-done = f32[2,4,3,3072]{3,0,2,1:T(2,128)} async-done(((f32[2,4,3,3072]{3,0,2,1:T(2,128)}), f32[2,4,3,3072]{3,0,2,1:T(2,128)}) %all-reduce.3.cloned.1.call-update) | async-done | bytes 294928
  109.6 1.7 dynamic-slice_bitcast_fusion.1
  111.3 0.7 copy.21
  112.0 3.3 %all-to-all-start.1 = ((f32[2,1,1,3,3072]{4,3,2,1,0:T(4,128)}), f32[2,1,1,3,3072]{4,3,2,1,0:T(4,128)S(1)}, u32[]{:S(2)}, u32[]{:S(2)}) async-start(f32[2,1,1,3,3072]{4,3,2,1,0:T(4,128)} %copy.21), calls=%async_computation.2 | async-start | bytes 196608 | tf_op jit(solution)/shard_map/all_to_all | solution.py:44
  115.4 0.1 convolution_bitcast_fusion
  115.6 4.0 %all-to-all-done.1 = f32[2,1,1,3,3072]{4,3,2,1,0:T(4,128)S(1)} async-done(((f32[2,1,1,3,3072]{4,3,2,1,0:T(4,128)}), f32[2,1,1,3,3072]{4,3,2,1,0:T(4,128)S(1)}, u32[]{:S(2)}, u32[]{:S(2)}) %all-to-all-start.1) | async-done | bytes 73760 | tf_op jit(solution)/shard_map/all_to_all | solution.py:44
  119.7 1.2 fusion.15
  120.9 52.7 %reduce-scatter.5.cloned.1.call-done = f32[16,384]{1,0:T(8,128)} async-done(((f32[16,6144]{1,0:T(8,128)}), f32[16,384]{1,0:T(8,128)}) %reduce-scatter.5.cloned.1.call-update) | async-done | bytes 24592 | tf_op jit(solution)/shard_map/reduce_scatter | solution.py:53
  173.6 1.3 convert_element_type.25
  (27 shorter events, 0.6 us)
Async XLA Ops:
  6.5 1.0 copy-start
  6.5 49.1 %reduce-scatter.3.cloned.1.call-start = ((), (), s32[]{:S(2)}) async-start(), calls=%async_computation.4 | async-start | bytes 1179648 | tf_op jit(solution)/shard_map/reduce_scatter | solution.py:31
  26.7 11.0 %copy-start.4 = (u32[32]{0:T(128)S(1)}, u32[32]{0:T(128)}, u32[]{:S(2)}) copy-start(u32[32]{0:T(128)} %constant.30) | copy-start | bytes 388
  26.7 11.6 %copy-start.3 = (s32[16,2]{0,1:T(2,128)S(1)}, s32[16,2]{0,1:T(2,128)}, u32[]{:S(2)}) copy-start(s32[16,2]{0,1:T(2,128)} %param.8) | copy-start | bytes 388
  26.7 148.3 %copy-start.1 = (bf16[16,6144]{1,0:T(8,128)(2,1)S(1)}, bf16[16,6144]{1,0:T(8,128)(2,1)}, u32[]{:S(2)}) copy-start(bf16[16,6144]{1,0:T(8,128)(2,1)} %param.6) | copy-start | bytes 589828
  36.7 36.8 %copy-start.2 = (s32[16,2]{0,1:T(2,128)S(1)}, s32[16,2]{0,1:T(2,128)}, u32[]{:S(2)}) copy-start(s32[16,2]{0,1:T(2,128)} %param.7) | copy-start | bytes 388
  37.6 71.9 %all-reduce.3.cloned.1.call-start = ((), (), s32[]{:S(2)}) async-start(), calls=%async_computation.6 | async-start | bytes 589824
  112.0 7.6 %all-to-all-start.1 = ((f32[2,1,1,3,3072]{4,3,2,1,0:T(4,128)}), f32[2,1,1,3,3072]{4,3,2,1,0:T(4,128)S(1)}, u32[]{:S(2)}, u32[]{:S(2)}) async-start(f32[2,1,1,3,3072]{4,3,2,1,0:T(4,128)} %copy.21), calls=%async_computation.2 | async-start | bytes 196608 | tf_op jit(solution)/shard_map/all_to_all | solution.py:44
  115.3 58.3 %reduce-scatter.5.cloned.1.call-start = ((), (), s32[]{:S(2)}) async-start(), calls=%async_computation.5 | async-start | bytes 417792 | tf_op jit(solution)/shard_map/reduce_scatter | solution.py:53
Sparse Core Ops, SparseCore 0:
  37.8 17.8 reduce-scatter.2
  73.6 35.9 all-reduce.2
  121.0 52.5 reduce-scatter.4
